TPU v7x, 256 devices: a whole 4x4x8 slice. The times are simulated.
256 devices in a mesh: row: 32 (over z, y), col: 8 (over x, core).
Axes of the slice: x: 4, y: 4, z: 8, core: 2. Of those that a mesh axis runs over, the one named last changes fastest.
Arguments:
- weights: float32 [2, 1, 8192, 4, 2048], P(None, None, 'row', None, 'col'), may hold values from -6 to 6
Outputs:
- trailing: float32 [2, 1, 8192, 4, 2048], P(None, None, 'row', None, 'col')
- diagonal: float32 [2, 12], replicated
- superdiag: float32 [2, 12], replicated
All inputs are finite; a program needn't handle non-finite values.
Results may differ from a plain program's by a relative error of at most 0.0003.
Values sent between devices are 32-bit elements; how exact they have to be, the bound alone decides.
No kernel may reach another device: no remote copies, remote signals or barrier semaphores. Data moves between devices by JAX's collectives and lax.ppermute only.
A program may use at most 64 MiB of HBM per device.

v0:
```python
import jax
import jax.numpy as jnp
from jax import lax
from jax.sharding import PartitionSpec as P

STEPS = 6
PANELS = 2


def picked(x, axis, root):
    return lax.dynamic_index_in_dim(lax.all_gather(x, axis), root, 0, keepdims=False)


def from_everyone(x, axis):
    copies = jnp.broadcast_to(x, (lax.axis_size(axis), *x.shape))
    return lax.all_to_all(copies, axis, split_axis=0, concat_axis=0, tiled=True)


def over_copies(x, axis):
    return from_everyone(x, axis).sum(axis=0)


def together(arrays, axis):
    ends = [0]
    for a in arrays:
        ends.append(ends[-1] + a.size)
    subtotal = over_copies(jnp.concatenate([a.ravel() for a in arrays]), axis)
    return tuple((subtotal[b:e].reshape(a.shape) for a, b, e in zip(arrays, ends, ends[1:])))


def contract(form, left, right):
    return jnp.einsum(form, left, right, precision=lax.Precision.HIGHEST)


def reflect(leading, squares):
    length = jnp.sqrt(squares)
    divisor = jnp.maximum(leading + length, 1.0)
    factor = (leading + length) / jnp.maximum(length, 1.0)
    return (divisor, factor, -length)


def placed(global_at, devices, tile_len):
    owner = global_at // tile_len % devices
    local_at = global_at // (devices * tile_len) * tile_len + global_at % tile_len
    return (owner, local_at)


def panel_merged(
    mats, grow, gcol, first_at, row_devices, col_devices, tile_len, row_place, col_place
):
    batch_n, local_rows, local_cols = mats.shape
    col_refl = jnp.zeros((batch_n, STEPS, local_rows), jnp.float32)
    col_aux = jnp.zeros((batch_n, STEPS, local_rows), jnp.float32)
    row_aux = jnp.zeros((batch_n, STEPS, local_cols), jnp.float32)
    row_refl = jnp.zeros((batch_n, STEPS, local_cols), jnp.float32)
    diag_list = []
    super_list = []
    start_owner, start_local = placed(first_at, col_devices, tile_len)
    pivot_col = picked(mats[:, :, start_local], "col", start_owner)
    aux_at = jnp.zeros((batch_n, STEPS), jnp.float32)
    refl_at = jnp.zeros((batch_n, STEPS), jnp.float32)
    for step_at in range(STEPS):
        pivot = first_at + step_at
        row_owner, row_local = placed(pivot, row_devices, tile_len)
        next_owner, next_local = placed(pivot + 1, col_devices, tile_len)
        col_piece = (
            pivot_col
            - contract("mp,mpr->mr", aux_at, col_refl)
            - contract("mp,mpr->mr", refl_at, col_aux)
        )
        col_piece = jnp.where(grow >= pivot, col_piece, 0.0)
        own_row = row_place == row_owner
        summed = together(
            (
                contract("mrc,mr->mc", mats, col_piece),
                contract("mpr,mr->mp", col_refl, col_piece),
                contract("mpr,mr->mp", col_aux, col_piece),
                jnp.sum(col_piece * col_piece, axis=1),
                jnp.sum(jnp.where(grow == pivot, col_piece, 0.0), axis=1),
                jnp.where(own_row, mats[:, row_local, :], 0.0),
                jnp.where(own_row, col_refl[:, :, row_local], 0.0),
                jnp.where(own_row, col_aux[:, :, row_local], 0.0),
            ),
            "row",
        )
        trans_piece, refl_dots, aux_dots, squares, leading, pivot_row, refl_row, aux_row = summed
        divisor, factor, bidiag = reflect(leading, squares)
        remain = (1.0 - leading / divisor)[:, None]
        col_vec = jnp.where(grow == pivot, 1.0, col_piece / divisor[:, None])
        transposed = trans_piece / divisor[:, None] + pivot_row * remain
        weighs_one = refl_dots / divisor[:, None] + refl_row * remain
        weighs_two = aux_dots / divisor[:, None] + aux_row * remain
        col_refl = col_refl.at[:, step_at].set(col_vec)
        col_img = factor[:, None] * (
            transposed
            - contract("mp,mpc->mc", weighs_one, row_aux)
            - contract("mp,mpc->mc", weighs_two, row_refl)
        )
        col_img = jnp.where(gcol > pivot, col_img, 0.0)
        row_aux = row_aux.at[:, step_at].set(col_img)
        refl_row = refl_row.at[:, step_at].set(1.0)
        row_piece = (
            pivot_row
            - contract("mp,mpc->mc", refl_row, row_aux)
            - contract("mp,mpc->mc", aux_row, row_refl)
        )
        row_piece = jnp.where(gcol > pivot, row_piece, 0.0)
        own_col = col_place == next_owner
        gathered = together(
            (
                contract("mrc,mc->mr", mats, row_piece),
                contract("mpc,mc->mp", row_aux, row_piece),
                contract("mpc,mc->mp", row_refl, row_piece),
                jnp.sum(row_piece * row_piece, axis=1),
                jnp.sum(jnp.where(gcol == pivot + 1, row_piece, 0.0), axis=1),
                jnp.where(own_col, mats[:, :, next_local], 0.0),
                jnp.where(own_col, row_aux[:, :, next_local], 0.0),
                jnp.where(own_col, row_refl[:, :, next_local], 0.0),
            ),
            "col",
        )
        apply_piece, aux_proj, refl_proj, squares2, leading2, next_col, next_aux, next_refl = (
            gathered
        )
        divisor2, factor2, bidiag2 = reflect(leading2, squares2)
        remain2 = (1.0 - leading2 / divisor2)[:, None]
        row_vec = jnp.where(gcol == pivot + 1, 1.0, row_piece / divisor2[:, None])
        applied = apply_piece / divisor2[:, None] + next_col * remain2
        dots_one = aux_proj / divisor2[:, None] + next_aux * remain2
        dots_two = refl_proj / divisor2[:, None] + next_refl * remain2
        row_refl = row_refl.at[:, step_at].set(row_vec)
        row_img = factor2[:, None] * (
            applied
            - contract("mp,mpr->mr", dots_one, col_refl)
            - contract("mp,mpr->mr", dots_two, col_aux)
        )
        row_img = jnp.where(grow > pivot, row_img, 0.0)
        col_aux = col_aux.at[:, step_at].set(row_img)
        diag_list.append(bidiag)
        super_list.append(bidiag2)
        pivot_col = next_col
        aux_at = next_aux
        refl_at = next_refl.at[:, step_at].set(1.0)
    return (col_refl, col_aux, row_aux, row_refl, diag_list, super_list)


def per_device(weights):
    batch_n, row_cycles, tile_len, col_cycles, _ = weights.shape
    local_rows = row_cycles * tile_len
    local_cols = col_cycles * tile_len
    mats = weights.reshape(batch_n, local_rows, local_cols)
    row_devices = lax.axis_size("row")
    col_devices = lax.axis_size("col")
    row_place = lax.axis_index("row")
    col_place = lax.axis_index("col")
    row_ids = jnp.arange(local_rows, dtype=jnp.int32)
    col_ids = jnp.arange(local_cols, dtype=jnp.int32)
    grow = (
        row_ids // tile_len * (row_devices * tile_len) + row_place * tile_len + row_ids % tile_len
    )
    gcol = (
        col_ids // tile_len * (col_devices * tile_len) + col_place * tile_len + col_ids % tile_len
    )
    diag_all = []
    super_all = []
    for panel_at in range(PANELS):
        first_at = panel_at * STEPS
        result = panel_merged(
            mats, grow, gcol, first_at, row_devices, col_devices, tile_len, row_place, col_place
        )
        col_refl, col_aux, row_aux, row_refl, diag_list, super_list = result
        mats = (
            mats
            - contract("mpr,mpc->mrc", col_refl, row_aux)
            - contract("mpr,mpc->mrc", col_aux, row_refl)
        )
        diag_all = diag_all + diag_list
        super_all = super_all + super_list
    done = PANELS * STEPS
    inside = (grow[:, None] >= done) & (gcol[None, :] >= done)
    trailing = jnp.where(inside[None], mats, 0.0).reshape(weights.shape)
    return (trailing, jnp.stack(diag_all, axis=1), jnp.stack(super_all, axis=1))


def solution(mesh):
    placed = (P(None, None, "row", None, "col"),)
    return jax.shard_map(
        per_device,
        mesh=mesh,
        in_specs=placed,
        out_specs=(P(None, None, "row", None, "col"), P(), P()),
        check_vma=False,
    )
```

profile of v0, /device:TPU:1, one launch (start us, length us, event | category | flops | bytes accessed | tf_op | source)
XLA Modules:
  0.0 568.3 jit_solution(11736387847308005558)
XLA Ops:
  0.6 2.3 reshape.3064
  4.0 14.3 %all-gather = f32[16,256,1]{1,2,0:T(1,128)S(1)} all-gather(f32[2,256,1]{1,2,0:T(1,128)S(1)} %copy.318), channel_id=2, replica_groups=mesh['row'=32,'col'=8] {'col'}, dimensions={0}, use_global_device_ids=true | all-gather | bytes 18432 | tf_op jit(solution)/shard_map/all_gather | solution.py:11
  21.2 10.2 %all-to-all-start = ((f32[32,1,4148]{2,1,0:T(1,128)}), f32[32,1,4148]{2,1,0:T(1,128)S(1)}, u32[]{:S(2)}, u32[]{:S(2)}) async-start(f32[32,1,4148]{2,1,0:T(1,128)} %broadcast_in_dim.644), calls=%async_computation | async-start | bytes 1081344 | tf_op jit(solution)/shard_map/all_to_all | solution.py:16
  32.2 16.3 %all-to-all-done = f32[32,1,4148]{2,1,0:T(1,128)S(1)} async-done(((f32[32,1,4148]{2,1,0:T(1,128)}), f32[32,1,4148]{2,1,0:T(1,128)S(1)}, u32[]{:S(2)}, u32[]{:S(2)}) %all-to-all-start) | async-done | bytes 530976 | tf_op jit(solution)/shard_map/all_to_all | solution.py:16
  54.8 5.3 all-to-all-start.1
  60.4 4.5 all-to-all-done.1
  70.2 4.4 all-to-all-start.2
  75.7 15.5 %all-to-all-done.2 = f32[32,1,4148]{2,1,0:T(1,128)S(1)} async-done(((f32[32,1,4148]{2,1,0:T(1,128)}), f32[32,1,4148]{2,1,0:T(1,128)S(1)}, u32[]{:S(2)}, u32[]{:S(2)}) %all-to-all-start.2) | async-done | bytes 530976 | tf_op jit(solution)/shard_map/all_to_all | solution.py:16
  94.8 1.8 fusion.463
  97.8 5.7 all-to-all-start.3
  103.7 4.5 all-to-all-done.3
  113.5 4.4 all-to-all-start.4
  118.3 16.2 %all-to-all-done.4 = f32[32,1,4148]{2,1,0:T(1,128)S(1)} async-done(((f32[32,1,4148]{2,1,0:T(1,128)}), f32[32,1,4148]{2,1,0:T(1,128)S(1)}, u32[]{:S(2)}, u32[]{:S(2)}) %all-to-all-start.4) | async-done | bytes 530976 | tf_op jit(solution)/shard_map/all_to_all | solution.py:16
  138.0 1.8 fusion.459
  141.0 5.7 all-to-all-start.5
  147.0 4.5 all-to-all-done.5
  156.9 4.4 all-to-all-start.6
  162.4 15.5 %all-to-all-done.6 = f32[32,1,4148]{2,1,0:T(1,128)S(1)} async-done(((f32[32,1,4148]{2,1,0:T(1,128)}), f32[32,1,4148]{2,1,0:T(1,128)S(1)}, u32[]{:S(2)}, u32[]{:S(2)}) %all-to-all-start.6) | async-done | bytes 530976 | tf_op jit(solution)/shard_map/all_to_all | solution.py:16
  181.6 1.8 fusion.455
  184.6 5.7 all-to-all-start.7
  190.5 4.5 all-to-all-done.7
  200.4 4.4 all-to-all-start.8
  205.2 16.2 %all-to-all-done.8 = f32[32,1,4148]{2,1,0:T(1,128)S(1)} async-done(((f32[32,1,4148]{2,1,0:T(1,128)}), f32[32,1,4148]{2,1,0:T(1,128)S(1)}, u32[]{:S(2)}, u32[]{:S(2)}) %all-to-all-start.8) | async-done | bytes 530976 | tf_op jit(solution)/shard_map/all_to_all | solution.py:16
  227.9 5.7 all-to-all-start.9
  233.8 4.5 all-to-all-done.9
  243.7 4.4 all-to-all-start.10
  248.5 16.2 %all-to-all-done.10 = f32[32,1,4148]{2,1,0:T(1,128)S(1)} async-done(((f32[32,1,4148]{2,1,0:T(1,128)}), f32[32,1,4148]{2,1,0:T(1,128)S(1)}, u32[]{:S(2)}, u32[]{:S(2)}) %all-to-all-start.10) | async-done | bytes 530976 | tf_op jit(solution)/shard_map/all_to_all | solution.py:16
  267.8 1.8 fusion.447
  270.9 5.7 all-to-all-start.11
  276.6 3.2 fusion.142
  282.5 4.1 subtract_subtract_fusion
  287.7 11.9 %all-gather.1 = f32[16,256,1]{1,2,0:T(1,128)S(1)} all-gather(f32[2,256,1]{1,2,0:T(1,128)S(1)} %copy.356), channel_id=3, replica_groups=mesh['row'=32,'col'=8] {'col'}, dimensions={0}, use_global_device_ids=true | all-gather | bytes 18432 | tf_op jit(solution)/shard_map/all_gather | solution.py:11
  302.4 4.4 all-to-all-start.12
  306.9 16.9 %all-to-all-done.12 = f32[32,1,4148]{2,1,0:T(1,128)S(1)} async-done(((f32[32,1,4148]{2,1,0:T(1,128)}), f32[32,1,4148]{2,1,0:T(1,128)S(1)}, u32[]{:S(2)}, u32[]{:S(2)}) %all-to-all-start.12) | async-done | bytes 530976 | tf_op jit(solution)/shard_map/all_to_all | solution.py:16
  327.0 1.9 fusion.467
  330.2 5.9 %all-to-all-start.13 = ((f32[8,1,1076]{2,1,0:T(1,128)}), f32[8,1,1076]{2,1,0:T(1,128)S(1)}, u32[]{:S(2)}, u32[]{:S(2)}) async-start(f32[8,1,1076]{2,1,0:T(1,128)} %broadcast_in_dim.694), calls=%async_computation.13 | async-start | bytes 73728 | tf_op jit(solution)/shard_map/all_to_all | solution.py:16
  336.4 4.4 all-to-all-done.13
  346.2 4.4 all-to-all-start.14
  351.1 16.2 %all-to-all-done.14 = f32[32,1,4148]{2,1,0:T(1,128)S(1)} async-done(((f32[32,1,4148]{2,1,0:T(1,128)}), f32[32,1,4148]{2,1,0:T(1,128)S(1)}, u32[]{:S(2)}, u32[]{:S(2)}) %all-to-all-start.14) | async-done | bytes 530976 | tf_op jit(solution)/shard_map/all_to_all | solution.py:16
  370.7 1.9 fusion.443
  373.7 5.7 all-to-all-start.15
  379.6 4.5 all-to-all-done.15
  389.6 4.4 all-to-all-start.16
  394.4 16.2 %all-to-all-done.16 = f32[32,1,4148]{2,1,0:T(1,128)S(1)} async-done(((f32[32,1,4148]{2,1,0:T(1,128)}), f32[32,1,4148]{2,1,0:T(1,128)S(1)}, u32[]{:S(2)}, u32[]{:S(2)}) %all-to-all-start.16) | async-done | bytes 530976 | tf_op jit(solution)/shard_map/all_to_all | solution.py:16
  414.1 1.9 fusion.439
  417.1 5.7 all-to-all-start.17
  423.0 4.5 all-to-all-done.17
  433.3 4.4 all-to-all-start.18
  438.1 16.2 %all-to-all-done.18 = f32[32,1,4148]{2,1,0:T(1,128)S(1)} async-done(((f32[32,1,4148]{2,1,0:T(1,128)}), f32[32,1,4148]{2,1,0:T(1,128)S(1)}, u32[]{:S(2)}, u32[]{:S(2)}) %all-to-all-start.18) | async-done | bytes 530976 | tf_op jit(solution)/shard_map/all_to_all | solution.py:16
  457.8 1.9 fusion.435
  460.8 5.7 all-to-all-start.19
  466.7 4.5 all-to-all-done.19
  476.7 4.4 all-to-all-start.20
  481.5 16.2 %all-to-all-done.20 = f32[32,1,4148]{2,1,0:T(1,128)S(1)} async-done(((f32[32,1,4148]{2,1,0:T(1,128)}), f32[32,1,4148]{2,1,0:T(1,128)S(1)}, u32[]{:S(2)}, u32[]{:S(2)}) %all-to-all-start.20) | async-done | bytes 530976 | tf_op jit(solution)/shard_map/all_to_all | solution.py:16
  501.2 1.9 fusion.431
  504.2 5.7 all-to-all-start.21
  510.2 4.5 all-to-all-done.21
  520.4 4.4 all-to-all-start.22
  527.4 14.0 %all-to-all-done.22 = f32[32,1,4148]{2,1,0:T(1,128)S(1)} async-done(((f32[32,1,4148]{2,1,0:T(1,128)}), f32[32,1,4148]{2,1,0:T(1,128)S(1)}, u32[]{:S(2)}, u32[]{:S(2)}) %all-to-all-start.22) | async-done | bytes 530976 | tf_op jit(solution)/shard_map/all_to_all | solution.py:16
  544.1 1.9 fusion.427
  547.2 5.7 all-to-all-start.23
  552.9 3.2 fusion.136
  558.9 5.1 subtract_select_fusion
  564.0 3.2 reshape.3329
  (918 shorter events, 136.6 us)
Async XLA Ops:
  3.0 264.8 %copy-start = (f32[2,256,1024]{2,1,0:T(8,128)}, f32[2,256,1024]{2,1,0:T(8,128)S(1)}, u32[]{:S(2)}) copy-start(f32[2,256,1024]{2,1,0:T(8,128)S(1)} %reshape.3064) | copy-start | bytes 6291460
  21.2 27.2 %all-to-all-start = ((f32[32,1,4148]{2,1,0:T(1,128)}), f32[32,1,4148]{2,1,0:T(1,128)S(1)}, u32[]{:S(2)}, u32[]{:S(2)}) async-start(f32[32,1,4148]{2,1,0:T(1,128)} %broadcast_in_dim.644), calls=%async_computation | async-start | bytes 1081344 | tf_op jit(solution)/shard_map/all_to_all | solution.py:16
  54.8 10.1 %all-to-all-start.1 = ((f32[8,1,1076]{2,1,0:T(1,128)}), f32[8,1,1076]{2,1,0:T(1,128)S(1)}, u32[]{:S(2)}, u32[]{:S(2)}) async-start(f32[8,1,1076]{2,1,0:T(1,128)} %broadcast_in_dim.651), calls=%async_computation.1 | async-start | bytes 73728 | tf_op jit(solution)/shard_map/all_to_all | solution.py:16
  70.2 21.0 %all-to-all-start.2 = ((f32[32,1,4148]{2,1,0:T(1,128)}), f32[32,1,4148]{2,1,0:T(1,128)S(1)}, u32[]{:S(2)}, u32[]{:S(2)}) async-start(f32[32,1,4148]{2,1,0:T(1,128)} %broadcast_in_dim.653), calls=%async_computation.2 | async-start | bytes 1081344 | tf_op jit(solution)/shard_map/all_to_all | solution.py:16
  97.8 10.4 %all-to-all-start.3 = ((f32[8,1,1076]{2,1,0:T(1,128)}), f32[8,1,1076]{2,1,0:T(1,128)S(1)}, u32[]{:S(2)}, u32[]{:S(2)}) async-start(f32[8,1,1076]{2,1,0:T(1,128)} %broadcast_in_dim.659), calls=%async_computation.3 | async-start | bytes 73728 | tf_op jit(solution)/shard_map/all_to_all | solution.py:16
  113.5 21.0 %all-to-all-start.4 = ((f32[32,1,4148]{2,1,0:T(1,128)}), f32[32,1,4148]{2,1,0:T(1,128)S(1)}, u32[]{:S(2)}, u32[]{:S(2)}) async-start(f32[32,1,4148]{2,1,0:T(1,128)} %broadcast_in_dim.661), calls=%async_computation.4 | async-start | bytes 1081344 | tf_op jit(solution)/shard_map/all_to_all | solution.py:16
  141.0 10.4 %all-to-all-start.5 = ((f32[8,1,1076]{2,1,0:T(1,128)}), f32[8,1,1076]{2,1,0:T(1,128)S(1)}, u32[]{:S(2)}, u32[]{:S(2)}) async-start(f32[8,1,1076]{2,1,0:T(1,128)} %broadcast_in_dim.666), calls=%async_computation.5 | async-start | bytes 73728 | tf_op jit(solution)/shard_map/all_to_all | solution.py:16
  156.9 21.0 %all-to-all-start.6 = ((f32[32,1,4148]{2,1,0:T(1,128)}), f32[32,1,4148]{2,1,0:T(1,128)S(1)}, u32[]{:S(2)}, u32[]{:S(2)}) async-start(f32[32,1,4148]{2,1,0:T(1,128)} %broadcast_in_dim.668), calls=%async_computation.6 | async-start | bytes 1081344 | tf_op jit(solution)/shard_map/all_to_all | solution.py:16
  184.6 10.4 %all-to-all-start.7 = ((f32[8,1,1076]{2,1,0:T(1,128)}), f32[8,1,1076]{2,1,0:T(1,128)S(1)}, u32[]{:S(2)}, u32[]{:S(2)}) async-start(f32[8,1,1076]{2,1,0:T(1,128)} %broadcast_in_dim.673), calls=%async_computation.7 | async-start | bytes 73728 | tf_op jit(solution)/shard_map/all_to_all | solution.py:16
  200.4 21.0 %all-to-all-start.8 = ((f32[32,1,4148]{2,1,0:T(1,128)}), f32[32,1,4148]{2,1,0:T(1,128)S(1)}, u32[]{:S(2)}, u32[]{:S(2)}) async-start(f32[32,1,4148]{2,1,0:T(1,128)} %broadcast_in_dim.675), calls=%async_computation.8 | async-start | bytes 1081344 | tf_op jit(solution)/shard_map/all_to_all | solution.py:16
  227.9 10.4 %all-to-all-start.9 = ((f32[8,1,1076]{2,1,0:T(1,128)}), f32[8,1,1076]{2,1,0:T(1,128)S(1)}, u32[]{:S(2)}, u32[]{:S(2)}) async-start(f32[8,1,1076]{2,1,0:T(1,128)} %broadcast_in_dim.680), calls=%async_computation.9 | async-start | bytes 73728 | tf_op jit(solution)/shard_map/all_to_all | solution.py:16
  243.7 21.0 %all-to-all-start.10 = ((f32[32,1,4148]{2,1,0:T(1,128)}), f32[32,1,4148]{2,1,0:T(1,128)S(1)}, u32[]{:S(2)}, u32[]{:S(2)}) async-start(f32[32,1,4148]{2,1,0:T(1,128)} %broadcast_in_dim.682), calls=%async_computation.10 | async-start | bytes 1081344 | tf_op jit(solution)/shard_map/all_to_all | solution.py:16
  270.9 10.4 %all-to-all-start.11 = ((f32[8,1,1076]{2,1,0:T(1,128)}), f32[8,1,1076]{2,1,0:T(1,128)S(1)}, u32[]{:S(2)}, u32[]{:S(2)}) async-start(f32[8,1,1076]{2,1,0:T(1,128)} %broadcast_in_dim.686), calls=%async_computation.11 | async-start | bytes 73728 | tf_op jit(solution)/shard_map/all_to_all | solution.py:16
  302.4 21.4 %all-to-all-start.12 = ((f32[32,1,4148]{2,1,0:T(1,128)}), f32[32,1,4148]{2,1,0:T(1,128)S(1)}, u32[]{:S(2)}, u32[]{:S(2)}) async-start(f32[32,1,4148]{2,1,0:T(1,128)} %broadcast_in_dim.689), calls=%async_computation.12 | async-start | bytes 1081344 | tf_op jit(solution)/shard_map/all_to_all | solution.py:16
  330.2 10.6 %all-to-all-start.13 = ((f32[8,1,1076]{2,1,0:T(1,128)}), f32[8,1,1076]{2,1,0:T(1,128)S(1)}, u32[]{:S(2)}, u32[]{:S(2)}) async-start(f32[8,1,1076]{2,1,0:T(1,128)} %broadcast_in_dim.694), calls=%async_computation.13 | async-start | bytes 73728 | tf_op jit(solution)/shard_map/all_to_all | solution.py:16
  346.2 21.0 %all-to-all-start.14 = ((f32[32,1,4148]{2,1,0:T(1,128)}), f32[32,1,4148]{2,1,0:T(1,128)S(1)}, u32[]{:S(2)}, u32[]{:S(2)}) async-start(f32[32,1,4148]{2,1,0:T(1,128)} %broadcast_in_dim.696), calls=%async_computation.14 | async-start | bytes 1081344 | tf_op jit(solution)/shard_map/all_to_all | solution.py:16
  373.7 10.4 %all-to-all-start.15 = ((f32[8,1,1076]{2,1,0:T(1,128)}), f32[8,1,1076]{2,1,0:T(1,128)S(1)}, u32[]{:S(2)}, u32[]{:S(2)}) async-start(f32[8,1,1076]{2,1,0:T(1,128)} %broadcast_in_dim.701), calls=%async_computation.15 | async-start | bytes 73728 | tf_op jit(solution)/shard_map/all_to_all | solution.py:16
  389.6 21.0 %all-to-all-start.16 = ((f32[32,1,4148]{2,1,0:T(1,128)}), f32[32,1,4148]{2,1,0:T(1,128)S(1)}, u32[]{:S(2)}, u32[]{:S(2)}) async-start(f32[32,1,4148]{2,1,0:T(1,128)} %broadcast_in_dim.703), calls=%async_computation.16 | async-start | bytes 1081344 | tf_op jit(solution)/shard_map/all_to_all | solution.py:16
  417.1 10.4 %all-to-all-start.17 = ((f32[8,1,1076]{2,1,0:T(1,128)}), f32[8,1,1076]{2,1,0:T(1,128)S(1)}, u32[]{:S(2)}, u32[]{:S(2)}) async-start(f32[8,1,1076]{2,1,0:T(1,128)} %broadcast_in_dim.708), calls=%async_computation.17 | async-start | bytes 73728 | tf_op jit(solution)/shard_map/all_to_all | solution.py:16
  433.3 21.0 %all-to-all-start.18 = ((f32[32,1,4148]{2,1,0:T(1,128)}), f32[32,1,4148]{2,1,0:T(1,128)S(1)}, u32[]{:S(2)}, u32[]{:S(2)}) async-start(f32[32,1,4148]{2,1,0:T(1,128)} %broadcast_in_dim.710), calls=%async_computation.18 | async-start | bytes 1081344 | tf_op jit(solution)/shard_map/all_to_all | solution.py:16
  460.8 10.4 %all-to-all-start.19 = ((f32[8,1,1076]{2,1,0:T(1,128)}), f32[8,1,1076]{2,1,0:T(1,128)S(1)}, u32[]{:S(2)}, u32[]{:S(2)}) async-start(f32[8,1,1076]{2,1,0:T(1,128)} %broadcast_in_dim.715), calls=%async_computation.19 | async-start | bytes 73728 | tf_op jit(solution)/shard_map/all_to_all | solution.py:16
  476.7 21.0 %all-to-all-start.20 = ((f32[32,1,4148]{2,1,0:T(1,128)}), f32[32,1,4148]{2,1,0:T(1,128)S(1)}, u32[]{:S(2)}, u32[]{:S(2)}) async-start(f32[32,1,4148]{2,1,0:T(1,128)} %broadcast_in_dim.717), calls=%async_computation.20 | async-start | bytes 1081344 | tf_op jit(solution)/shard_map/all_to_all | solution.py:16
  504.2 10.4 %all-to-all-start.21 = ((f32[8,1,1076]{2,1,0:T(1,128)}), f32[8,1,1076]{2,1,0:T(1,128)S(1)}, u32[]{:S(2)}, u32[]{:S(2)}) async-start(f32[8,1,1076]{2,1,0:T(1,128)} %broadcast_in_dim.722), calls=%async_computation.21 | async-start | bytes 73728 | tf_op jit(solution)/shard_map/all_to_all | solution.py:16
  520.4 21.0 %all-to-all-start.22 = ((f32[32,1,4148]{2,1,0:T(1,128)}), f32[32,1,4148]{2,1,0:T(1,128)S(1)}, u32[]{:S(2)}, u32[]{:S(2)}) async-start(f32[32,1,4148]{2,1,0:T(1,128)} %broadcast_in_dim.724), calls=%async_computation.22 | async-start | bytes 1081344 | tf_op jit(solution)/shard_map/all_to_all | solution.py:16
  547.2 10.4 %all-to-all-start.23 = ((f32[8,1,1076]{2,1,0:T(1,128)}), f32[8,1,1076]{2,1,0:T(1,128)S(1)}, u32[]{:S(2)}, u32[]{:S(2)}) async-start(f32[8,1,1076]{2,1,0:T(1,128)} %broadcast_in_dim.728), calls=%async_computation.23 | async-start | bytes 73728 | tf_op jit(solution)/shard_map/all_to_all | solution.py:16
where the time goes:
time: 578 us; the launch traced here: 568 us
  waiting for transfers between devices  239 us (41%)
  starting transfers between devices  127 us (22%)
  matrix products  76.1 us (13%)
  local copies, waits for them, and re-layouts  60.6 us (10%)
  other arithmetic  37.2 us (6%)
  blocking collectives  26.2 us (5%)
    all_to_all x24, waiting for transfers between devices, from_everyone(): return lax.all_to_all(copies, axis, split_axis=0, concat_axis=0, tiled=True)  239 us
    all_to_all x24, starting transfers between devices, from_everyone(): return lax.all_to_all(copies, axis, split_axis=0, concat_axis=0, tiled=True)  127 us
    dot_general x167, matrix products, contract(): return jnp.einsum(form, left, right, precision=lax.Precision.HIGHEST)  76.1 us
    all_gather x2, blocking collectives, picked(): lax.all_gather(x, axis)  26.2 us
    broadcast_in_dim x24, local copies, waits for them, and re-layouts, from_everyone(): copies = jnp.broadcast_to(x, (lax.axis_size(axis), *x.shape))  20.7 us
    another operation x31, other arithmetic  16.4 us
  transfers between devices with their start and end apart: 24, of which 24 were waited for; matrix products, arithmetic and copies ran while one was open for 3% of the time, Pallas kernels for 0%

commit v1 on v0

v1 whole, which is shorter than its diff:
```python
import functools

import jax
import jax.numpy as jnp
from jax import lax
from jax.experimental import pallas as pl
from jax.experimental.pallas import tpu as pltpu
from jax.sharding import PartitionSpec as P

TOTAL = 12
SLOTS = 16
LANES = 128
AT_SQUARES, AT_LEAD, AT_SECOND, AT_PICK, AT_PICK2 = 32, 33, 16, 64, 80
VMEM = pl.BlockSpec(memory_space=pltpu.VMEM)
F32 = jnp.float32


def spread(row):
    return jnp.transpose(jnp.broadcast_to(row, (LANES, LANES)))


def gather_lanes(rows):
    return jnp.sum(jnp.transpose(rows), axis=0, keepdims=True)


def total(x):
    return jnp.sum(x, axis=0, keepdims=True)


def wide(x, n):
    return jnp.concatenate([x] * n, axis=1)


def fold(x):
    return sum(x[:, at : at + LANES] for at in range(0, x.shape[1], LANES))


def dots_row(first, second, squares, lead, pick, pick2):
    at = lax.broadcasted_iota(jnp.int32, (SLOTS, LANES), 0)
    pair = jnp.where(at == 0, squares, jnp.where(at == 1, lead, 0.0))
    none = jnp.zeros((SLOTS, LANES), F32)
    return gather_lanes(jnp.concatenate([first, second, pair, none, pick, pick2, none, none], axis=0))


def reflect(dots):
    lead = dots[AT_LEAD : AT_LEAD + 1]
    length = jnp.sqrt(dots[AT_SQUARES : AT_SQUARES + 1])
    divisor = jnp.maximum(lead + length, 1.0)
    factor = (lead + length) / jnp.maximum(length, 1.0)
    return divisor, factor, 1.0 - lead / divisor, -length


def slot(ref, at):
    return ref.at[at : at + 1]


def tiles(ref):
    return [slice(at, at + LANES) for at in range(0, ref.shape[1], LANES)]


def finish_row_side(step, sums, r_ref, gr_ref, gc_ref, cols_ref, v_ref, x_ref, u_ref, sd_ref):
    rows = gr_ref.shape[1]
    dots = spread(sums[:, rows:])
    divisor, factor, remain, bidiag = reflect(dots)
    pick, pick2 = dots[AT_PICK : AT_PICK + SLOTS], dots[AT_PICK2 : AT_PICK2 + SLOTS]
    one = dots[:SLOTS] / divisor + pick * remain
    two = dots[AT_SECOND : AT_SECOND + SLOTS] / divisor + pick2 * remain
    n = rows // LANES
    col = cols_ref[step : step + 1]
    v, x = v_ref[...], x_ref[...]
    image = wide(factor, n) * (
        sums[:, :rows] / wide(divisor, n)
        + col * wide(remain, n)
        - total(wide(one, n) * v + wide(two, n) * x)
    )
    image = jnp.where(gr_ref[...] >= step, image, 0.0)
    column = col - total(wide(pick, n) * v + wide(pick2, n) * x) - image
    x_ref[step - 1 : step, :] = image
    sd_ref[step - 1 : step, :] = bidiag
    for ts in tiles(r_ref):
        u_ref[step - 1 : step, ts] = jnp.where(gc_ref[:, ts] == step, 1.0, r_ref[:, ts] / divisor)
    return jnp.where(gr_ref[...] >= step, column, 0.0)


def send_row(step, column, gr_ref, own_ref, oth_ref, v_ref, x_ref, msg_ref, c_ref, extra=None):
    rows = gr_ref.shape[1]
    c_ref[...] = column
    spread_c = jnp.transpose(jnp.broadcast_to(column, (LANES, rows)))
    parts = []
    for ref in (own_ref, oth_ref):
        for ts in tiles(ref):
            parts.append(total(ref[:, ts] * spread_c))
    hit = gr_ref[...] == step
    lead = fold(jnp.where(hit, column, 0.0))
    squares = fold(column * column)
    if v_ref is None:
        none = jnp.zeros((SLOTS, LANES), F32)
        parts.append(dots_row(none, none, squares, lead, none, none))
    else:
        v, x = v_ref[...], x_ref[...]
        parts.append(
            dots_row(
                fold(v * column),
                fold(x * column),
                squares,
                lead,
                fold(jnp.where(hit, v, 0.0)),
                fold(jnp.where(hit, x, 0.0)),
            )
        )
    if extra is not None:
        parts.append(extra)
    message = jnp.concatenate(parts, axis=1)
    for peer in range(msg_ref.shape[0]):
        msg_ref[peer] = message


def carry(before, after):
    for old, new in zip(before, after):
        new[...] = old[...]


def first_kernel(gr_ref, cols_ref, scat_ref, own_ref, oth_ref, msg_ref, c_ref, *state):
    for ref in state:
        ref[...] = jnp.zeros_like(ref)
    send_row(0, cols_ref[0:1], gr_ref, own_ref, oth_ref, None, None, msg_ref, c_ref, scat_ref[0])


def column_kernel(
    step, a_ref, b_ref, r_ref, gr_ref, gc_ref, cols_ref, own_ref, oth_ref, v_ref,
    x_in, u_in, sd_in, msg_ref, c_ref, x_ref, u_ref, sd_ref,
):
    carry((x_in, u_in, sd_in), (x_ref, u_ref, sd_ref))
    sums = a_ref[...] + b_ref[...]
    column = finish_row_side(
        step, sums, r_ref, gr_ref, gc_ref, cols_ref, v_ref, x_ref, u_ref, sd_ref
    )
    send_row(step, column, gr_ref, own_ref, oth_ref, v_ref, x_ref, msg_ref, c_ref)


def last_kernel(
    a_ref, b_ref, r_ref, gr_ref, gc_ref, cols_ref, v_ref, y_ref, dg_ref,
    x_in, u_in, sd_in, own_ref, oth_ref, x_ref, u_ref, sd_ref,
):
    carry((x_in, u_in, sd_in), (x_ref, u_ref, sd_ref))
    sums = a_ref[...] + b_ref[...]
    finish_row_side(TOTAL, sums, r_ref, gr_ref, gc_ref, cols_ref, v_ref, x_ref, u_ref, sd_ref)
    rows, half = gr_ref.shape[1], gc_ref.shape[1] // 2
    for ref, begin in ((own_ref, 0), (oth_ref, half)):
        ref[:SLOTS, :rows] = v_ref[...]
        ref[SLOTS:, :rows] = x_ref[...]
        ref[:SLOTS, rows : rows + half] = y_ref[:, begin : begin + half]
        ref[SLOTS:, rows : rows + half] = u_ref[:, begin : begin + half]
        ref[:SLOTS, rows + half :] = dg_ref[...]
        ref[SLOTS:, rows + half :] = sd_ref[...]


def row_kernel(
    step, recv_ref, c_ref, gr_ref, gc_ref, *refs,
):
    if step == 0:
        own_ref, oth_ref, u_ref, v_in, y_in, dg_in, msg_ref, r_ref, v_ref, y_ref, dg_ref, piv_ref = refs
    else:
        piv_ref, own_ref, oth_ref, u_ref, v_in, y_in, dg_in, msg_ref, r_ref, v_ref, y_ref, dg_ref = refs
    carry((v_in, y_in, dg_in), (v_ref, y_ref, dg_ref))
    cols = gc_ref.shape[1]
    summed = recv_ref[0, :, : cols + LANES]
    for peer in range(1, recv_ref.shape[0]):
        summed = summed + recv_ref[peer, :, : cols + LANES]
    if step == 0:
        piece = recv_ref.shape[2] - cols - LANES
        piv_ref[TOTAL:, :] = jnp.zeros((SLOTS - TOTAL, cols), F32)
        for peer in range(recv_ref.shape[0]):
            for at in range(0, piece, LANES):
                flat = peer * piece + at
                row, begin = flat // cols, flat % cols
                piv_ref[row : row + 1, begin : begin + LANES] = recv_ref[
                    peer, :, cols + LANES + at : cols + 2 * LANES + at
                ]
    dots = spread(summed[:, cols:])
    divisor, factor, remain, bidiag = reflect(dots)
    pick, pick2 = dots[AT_PICK : AT_PICK + SLOTS], dots[AT_PICK2 : AT_PICK2 + SLOTS]
    one = dots[:SLOTS] / divisor + pick * remain
    two = dots[AT_SECOND : AT_SECOND + SLOTS] / divisor + pick2 * remain
    dg_ref[step : step + 1, :] = bidiag
    n = gr_ref.shape[1] // LANES
    v_ref[step : step + 1, :] = jnp.where(gr_ref[...] == step, 1.0, c_ref[...] / wide(divisor, n))
    at_slot = lax.broadcasted_iota(jnp.int32, (SLOTS, LANES), 0) == step
    image = jnp.zeros((own_ref.shape[0], LANES), F32)
    first = second = pick_y = pick_u = jnp.zeros((SLOTS, LANES), F32)
    squares = lead = jnp.zeros((1, LANES), F32)
    half = cols // 2
    for begin in range(0, cols, LANES):
        ts = slice(begin, begin + LANES)
        y_t, u_t, piv_t, gc_t = y_ref[:, ts], u_ref[:, ts], piv_ref[step : step + 1, ts], gc_ref[:, ts]
        y = factor * (summed[:, ts] / divisor + piv_t * remain - total(one * y_t + two * u_t))
        y = jnp.where(gc_t > step, y, 0.0)
        r = piv_t - total(pick * y_t + pick2 * u_t) - y
        r = jnp.where(gc_t > step, r, 0.0)
        y_ref[step : step + 1, ts] = y
        r_ref[:, ts] = r
        y_t = jnp.where(at_slot, y, y_t)
        first, second, squares = first + y_t * r, second + u_t * r, squares + r * r
        if begin % half == 0:
            hit = gc_t == step + 1
            lead = lead + jnp.where(hit, r, 0.0)
            pick_y = pick_y + jnp.where(hit, y_t, 0.0)
            pick_u = pick_u + jnp.where(hit, u_t, 0.0)
        block = own_ref[:, ts] if begin < half else oth_ref[:, begin - half : begin - half + LANES]
        image = image + block * r
    msg_ref[...] = jnp.concatenate(
        [gather_lanes(image), dots_row(first, second, squares, lead, pick_y, pick_u)], axis=1
    )


def call(kernel, name, ins, outs):
    return pl.pallas_call(
        kernel,
        name=name,
        out_shape=[pltpu.VMEM(s, F32) for s in outs],
        in_specs=[VMEM] * len(ins),
        out_specs=[VMEM] * len(outs),
    )(*(pltpu.with_memory_space_constraint(x, pltpu.VMEM) for x in ins))


def per_device(weights):
    batch_n, row_cycles, tile_len, col_cycles, _ = weights.shape
    rows, cols = row_cycles * tile_len, col_cycles * tile_len
    w = weights.reshape(batch_n, rows, cols)
    row_devices, col_devices = lax.axis_size("row"), lax.axis_size("col")
    row_place, col_place = lax.axis_index("row"), lax.axis_index("col")
    core, chip = col_place % 2, col_place // 2
    chips = col_devices // 2
    everyone = range(col_devices)
    swap = [(i, i ^ 1) for i in everyone]
    near = [(i, i ^ 2) for i in everyone]
    far = [(i, 2 * (chips - 1 - i // 2) + i % 2) for i in everyone]

    col_ids = jnp.arange(cols, dtype=jnp.int32)

    def global_cols(place):
        return col_ids // tile_len * (col_devices * tile_len) + place * tile_len + col_ids % tile_len

    gcol = global_cols(col_place)
    gc = jnp.concatenate([gcol, global_cols(col_place ^ 1)])[None]
    grow = row_place * tile_len + jnp.arange(rows, dtype=jnp.int32)
    gr = grow[None]

    own = jnp.where(core == 0, w[0], w[1])
    oth = lax.ppermute(jnp.where(core == 0, w[1], w[0]), "col", swap)

    both = 2 * cols
    piece = TOTAL * both // row_devices
    scat = jnp.concatenate([own[:TOTAL], oth[:TOTAL]], axis=1).reshape(row_devices, 1, piece)
    scat = lax.all_to_all(scat, "row", split_axis=0, concat_axis=0, tiled=True)
    slab = jnp.where(core == 0, own[:, :SLOTS], oth[:, :SLOTS]).T
    slab = jnp.where(chip == 0, slab, 0.0)
    slab = slab + lax.ppermute(slab, "col", [(0, 2), (1, 3)])
    first_cols = slab + lax.ppermute(slab, "col", [(0, 6), (1, 7), (2, 4), (3, 5)])

    vec_r, vec_c, flag = (SLOTS, rows), (SLOTS, both), (SLOTS, LANES)
    msg = (row_devices, 1, both + LANES)
    msg_long = (row_devices, 1, both + LANES + piece)
    out = call(
        first_kernel,
        "first",
        (gr, first_cols, scat, own, oth),
        (msg_long, (1, rows), vec_r, vec_r, vec_c, vec_c, flag, flag),
    )
    message, column, v, x, y, u, dg, sd = out
    pivots = None
    for step in range(TOTAL):
        recv = lax.all_to_all(message, "row", split_axis=0, concat_axis=0, tiled=True)
        lead_in = (recv, column, gr, gc)
        state = (own, oth, u, v, y, dg)
        outs = ((1, rows + LANES), (1, both), vec_r, vec_c, flag)
        kernel = functools.partial(row_kernel, step)
        if step == 0:
            ins, outs = lead_in + state, outs + (vec_c,)
            message, r, v, y, dg, pivots = call(kernel, "row_step", ins, outs)
        else:
            ins = lead_in + (pivots,) + state
            message, r, v, y, dg = call(kernel, "row_step", ins, outs)
        part = message + lax.ppermute(message, "col", near)
        rest = lax.ppermute(part, "col", far)
        if step + 1 < TOTAL:
            ins = (part, rest, r, gr, gc, first_cols, own, oth, v, x, u, sd)
            message, column, x, u, sd = call(
                functools.partial(column_kernel, step + 1),
                "column_step",
                ins,
                (msg, (1, rows), vec_r, vec_c, flag),
            )
    ins = (part, rest, r, gr, gc, first_cols, v, y, dg, x, u, sd)
    packed = (2 * SLOTS, rows + cols + LANES)
    mine, theirs, _, _, _ = call(last_kernel, "last", ins, (packed, packed, vec_r, vec_c, flag))
    theirs = lax.ppermute(theirs, "col", swap)
    packs = jnp.stack(
        [jnp.where(core == 0, mine, theirs), jnp.where(core == 0, theirs, mine)]
    )
    change = jnp.einsum(
        "mpr,mpc->mrc",
        packs[:, :, :rows],
        packs[:, :, rows : rows + cols],
        precision=lax.Precision.HIGHEST,
    )
    inside = (grow[:, None] >= TOTAL) & (gcol[None, :] >= TOTAL)
    trailing = jnp.where(inside[None], w - change, 0.0).reshape(weights.shape)
    ends = packs[:, :, rows + cols]
    return trailing, ends[:, :TOTAL], ends[:, SLOTS : SLOTS + TOTAL]


def solution(mesh):
    placed = P(None, None, "row", None, "col")
    return jax.shard_map(
        per_device,
        mesh=mesh,
        in_specs=(placed,),
        out_specs=(placed, P(), P()),
        check_vma=False,
    )
```

time: 578 us -> 407 us (0.70); the launches traced: 568 us -> 404 us
  waiting for transfers between devices: 239 us -> 76.9 us
  blocking collectives: 26.2 us -> 158 us
  matrix products: 76.1 us -> 3.63 us
  starting transfers between devices: 127 us -> 81.5 us
  other arithmetic: 37.2 us -> 2.33 us
  Pallas kernels: 0 us -> 12 us
  local copies, waits for them, and re-layouts: 60.6 us -> 69.1 us
    all_to_all x24 -> x2, waiting for transfers between devices: 239 us -> 13.6 us  [the longest x1 12.2 us: per_device(): lax.all_to_all(message, 'row', split_axis=0, concat_axis=0, tiled=True)]
    all_to_all x0 -> x11, blocking collectives: none -> 158 us  [per_device(): lax.all_to_all(message, 'row', split_axis=0, concat_axis=0, tiled=True)]
    all_to_all x24 -> x2, starting transfers between devices: 127 us -> 17.3 us  [the longest x1 9.5 us: per_device(): scat = lax.all_to_all(scat, 'row', split_axis=0, concat_axis=0, tiled=True)]
    dot_general x167 -> x1, matrix products: 76.1 us -> 3.63 us  [per_device(): jnp.einsum('mpr,mpc->mrc', packs[:, :, :rows], packs[:, :, rows:rows + co...]
    ppermute x0 -> x28, starting transfers between devices: none -> 64.2 us  [the longest x1 43 us: per_device(): theirs = lax.ppermute(theirs, 'col', swap)]
    ppermute x0 -> x28, waiting for transfers between devices: none -> 63.3 us  [the longest x12 30.6 us: per_device(): rest = lax.ppermute(part, 'col', far)]
    unnamed x38 -> x107, local copies, waits for them, and re-layouts: 0.16 us -> 58.2 us
    all_gather x2 -> x0, blocking collectives: 26.2 us -> none  [picked(): lax.all_gather(x, axis)]
  transfers between devices with their start and end apart: 24 -> 30, of which waited for: 24 -> 28; matrix products, arithmetic and copies ran while one was open for 3% -> 2% of each run, Pallas kernels for 0% -> 0%
where the time goes in v1:
time: 407 us; the launch traced here: 404 us
  blocking collectives  158 us (39%)
  starting transfers between devices  81.5 us (20%)
  waiting for transfers between devices  76.9 us (19%)
  local copies, waits for them, and re-layouts  69.1 us (17%)
  Pallas kernels  12 us (3%)
    all_to_all x11, blocking collectives, per_device(): lax.all_to_all(message, 'row', split_axis=0, concat_axis=0, tiled=True)  158 us
    unnamed x107, local copies, waits for them, and re-layouts  58.2 us
    ppermute x1, starting transfers between devices, per_device(): theirs = lax.ppermute(theirs, 'col', swap)  43 us
    ppermute x12, waiting for transfers between devices, per_device(): rest = lax.ppermute(part, 'col', far)  30.6 us
    ppermute x12, waiting for transfers between devices, per_device(): part = message + lax.ppermute(message, 'col', near)  29 us
    all_to_all x1, waiting for transfers between devices, per_device(): lax.all_to_all(message, 'row', split_axis=0, concat_axis=0, tiled=True)  12.2 us
    pallas_call x25, Pallas kernels, call(): pl.pallas_call(kernel, name=name, out_shape=[pltpu.VMEM(s, F32) for s in...  12 us
    ppermute x12, starting transfers between devices, per_device(): rest = lax.ppermute(part, 'col', far)  11.1 us
  transfers between devices with their start and end apart: 30, of which 28 were waited for; matrix products, arithmetic and copies ran while one was open for 2% of the time, Pallas kernels for 0%

profile of v1, /device:TPU:1, one launch (start us, length us, event | category | flops | bytes accessed | tf_op | source)
XLA Modules:
  0.0 404.3 jit_solution(13816179352749544495)
XLA Ops:
  0.6 1.9 slice_select_fusion.1
  2.6 1.4 copy.111
  3.9 3.2 collective-permute-start
  7.6 2.0 collective-permute-done
  10.6 9.5 %all-to-all-start = ((f32[32,1,768]{2,1,0:T(1,128)}), f32[32,1,768]{2,1,0:T(1,128)S(1)}, u32[]{:S(2)}, u32[]{:S(2)}) async-start(f32[32,1,768]{2,1,0:T(1,128)} %reshape.92), calls=%async_computation | async-start | bytes 196608 | tf_op jit(solution)/shard_map/all_to_all | solution.py:255
  20.2 3.1 collective-permute-start.1
  24.1 1.3 collective-permute-start.2
  25.8 1.9 copy.115.oth_ref.refs_1_.refs_2_
  27.8 1.4 all-to-all-done.scat_ref
  30.3 7.8 %all-to-all-start.1 = ((f32[32,1,2944]{2,1,0:T(1,128)}), f32[32,1,2944]{2,1,0:T(1,128)S(1)}, u32[]{:S(2)}, u32[]{:S(2)}) async-start(f32[32,1,2944]{2,1,0:T(1,128)} %get-tuple-element.129), calls=%async_computation.1 | async-start | bytes 753664 | tf_op jit(solution)/shard_map/all_to_all | solution.py:273
  38.1 12.2 %all-to-all-done.1.recv_ref = f32[32,1,2944]{2,1,0:T(1,128)S(1)} async-done(((f32[32,1,2944]{2,1,0:T(1,128)}), f32[32,1,2944]{2,1,0:T(1,128)S(1)}, u32[]{:S(2)}, u32[]{:S(2)}) %all-to-all-start.1) | async-done | bytes 376864 | tf_op jit(solution)/shard_map/all_to_all | solution.py:273
  50.3 1.2 copy-done.1
  55.3 1.4 collective-permute-done.3
  57.2 3.1 collective-permute-done.4.b_ref
  60.3 1.2 copy-done.2
  64.0 16.1 %all_to_all.65.recv_ref = f32[32,1,2176]{2,1,0:T(1,128)S(1)} all-to-all(f32[32,1,2176]{2,1,0:T(1,128)S(1)} %get-tuple-element.140), channel_id=1, replica_groups=mesh['row'=32,'col'=8] {'row'}, dimensions={0} | all-to-all | bytes 557056 | tf_op jit(solution)/shard_map/all_to_all | solution.py:273
  80.1 1.2 copy-done.3
  83.3 2.3 collective-permute-done.5
  86.2 3.0 collective-permute-done.6.b_ref
  89.2 1.2 copy-done.4
  92.1 14.0 %all_to_all.66.recv_ref = f32[32,1,2176]{2,1,0:T(1,128)S(1)} all-to-all(f32[32,1,2176]{2,1,0:T(1,128)S(1)} %get-tuple-element.151), channel_id=1, replica_groups=mesh['row'=32,'col'=8] {'row'}, dimensions={0} | all-to-all | bytes 557056 | tf_op jit(solution)/shard_map/all_to_all | solution.py:273
  106.1 1.2 copy-done.5
  109.2 2.7 collective-permute-done.7
  112.5 3.0 collective-permute-done.8.b_ref
  115.5 1.2 copy-done.6
  118.4 13.9 %all_to_all.67.recv_ref = f32[32,1,2176]{2,1,0:T(1,128)S(1)} all-to-all(f32[32,1,2176]{2,1,0:T(1,128)S(1)} %get-tuple-element.161), channel_id=1, replica_groups=mesh['row'=32,'col'=8] {'row'}, dimensions={0} | all-to-all | bytes 557056 | tf_op jit(solution)/shard_map/all_to_all | solution.py:273
  132.3 1.2 copy-done.7
  135.5 2.7 collective-permute-done.9
  139.2 3.0 collective-permute-done.10.b_ref
  142.2 1.2 copy-done.8
  145.0 13.7 %all_to_all.68.recv_ref = f32[32,1,2176]{2,1,0:T(1,128)S(1)} all-to-all(f32[32,1,2176]{2,1,0:T(1,128)S(1)} %get-tuple-element.171), channel_id=1, replica_groups=mesh['row'=32,'col'=8] {'row'}, dimensions={0} | all-to-all | bytes 557056 | tf_op jit(solution)/shard_map/all_to_all | solution.py:273
  158.8 1.2 copy-done.9
  161.8 2.4 collective-permute-done.11
  165.1 2.9 collective-permute-done.12.b_ref
  168.0 1.2 copy-done.10
  170.8 13.9 %all_to_all.69.recv_ref = f32[32,1,2176]{2,1,0:T(1,128)S(1)} all-to-all(f32[32,1,2176]{2,1,0:T(1,128)S(1)} %get-tuple-element.181), channel_id=1, replica_groups=mesh['row'=32,'col'=8] {'row'}, dimensions={0} | all-to-all | bytes 557056 | tf_op jit(solution)/shard_map/all_to_all | solution.py:273
  184.7 1.2 copy-done.11
  187.7 2.4 collective-permute-done.13
  191.0 2.8 collective-permute-done.14.b_ref
  193.8 1.2 copy-done.12
  196.6 13.9 %all_to_all.70.recv_ref = f32[32,1,2176]{2,1,0:T(1,128)S(1)} all-to-all(f32[32,1,2176]{2,1,0:T(1,128)S(1)} %get-tuple-element.191), channel_id=1, replica_groups=mesh['row'=32,'col'=8] {'row'}, dimensions={0} | all-to-all | bytes 557056 | tf_op jit(solution)/shard_map/all_to_all | solution.py:273
  213.6 2.4 collective-permute-done.15
  216.9 2.8 collective-permute-done.16.b_ref
  222.5 14.2 %all_to_all.71.recv_ref = f32[32,1,2176]{2,1,0:T(1,128)S(1)} all-to-all(f32[32,1,2176]{2,1,0:T(1,128)S(1)} %get-tuple-element.201), channel_id=1, replica_groups=mesh['row'=32,'col'=8] {'row'}, dimensions={0} | all-to-all | bytes 557056 | tf_op jit(solution)/shard_map/all_to_all | solution.py:273
  239.7 2.4 collective-permute-done.17
  242.2 1.4 collective-permute-start.18
  243.6 2.2 collective-permute-done.18.b_ref
  248.7 15.3 %all_to_all.72.recv_ref = f32[32,1,2176]{2,1,0:T(1,128)S(1)} all-to-all(f32[32,1,2176]{2,1,0:T(1,128)S(1)} %get-tuple-element.211), channel_id=1, replica_groups=mesh['row'=32,'col'=8] {'row'}, dimensions={0} | all-to-all | bytes 557056 | tf_op jit(solution)/shard_map/all_to_all | solution.py:273
  267.0 2.4 collective-permute-done.19
  270.1 2.9 collective-permute-done.20.b_ref
  275.9 14.8 %all_to_all.73.recv_ref = f32[32,1,2176]{2,1,0:T(1,128)S(1)} all-to-all(f32[32,1,2176]{2,1,0:T(1,128)S(1)} %get-tuple-element.221), channel_id=1, replica_groups=mesh['row'=32,'col'=8] {'row'}, dimensions={0} | all-to-all | bytes 557056 | tf_op jit(solution)/shard_map/all_to_all | solution.py:273
  293.7 2.4 collective-permute-done.21
  297.3 2.5 collective-permute-done.22.b_ref
  302.6 13.9 %all_to_all.74.recv_ref = f32[32,1,2176]{2,1,0:T(1,128)S(1)} all-to-all(f32[32,1,2176]{2,1,0:T(1,128)S(1)} %get-tuple-element.231), channel_id=1, replica_groups=mesh['row'=32,'col'=8] {'row'}, dimensions={0} | all-to-all | bytes 557056 | tf_op jit(solution)/shard_map/all_to_all | solution.py:273
  319.6 2.7 collective-permute-done.23
  322.3 1.3 collective-permute-start.24
  323.5 2.4 collective-permute-done.24.b_ref
  328.8 13.9 %all_to_all.75.recv_ref = f32[32,1,2176]{2,1,0:T(1,128)S(1)} all-to-all(f32[32,1,2176]{2,1,0:T(1,128)S(1)} %get-tuple-element.241), channel_id=1, replica_groups=mesh['row'=32,'col'=8] {'row'}, dimensions={0} | all-to-all | bytes 557056 | tf_op jit(solution)/shard_map/all_to_all | solution.py:273
  345.8 2.7 collective-permute-done.25
  348.5 1.3 collective-permute-start.26
  349.7 3.3 reshape.89
  353.8 43.0 %collective-permute-start.27 = (f32[32,1408]{1,0:T(8,128)S(1)}, f32[32,1408]{1,0:T(8,128)S(1)}, u32[]{:S(2)}, u32[]{:S(2)}) collective-permute-start(f32[32,1408]{1,0:T(8,128)S(1)} %get-tuple-element.254), channel_id=1, source_target_pairs={{0,1},{1,0},{2,3},{3,2},{4,5},{5,4},{6,7},{7,6},{8,9},{9,8},{10,11... | collective-permute-start | bytes 540680 | tf_op jit(solution)/shard_map/ppermute | solution.py:297
  398.6 3.6 subtract_select_fusion
  402.3 2.0 reshape.91
  (175 shorter events, 69.7 us)
Async XLA Ops:
  3.9 5.7 %collective-permute-start = (f32[256,1024]{0,1:T(8,128)}, f32[256,1024]{0,1:T(8,128)S(1)}, u32[]{:S(2)}, u32[]{:S(2)}) collective-permute-start(f32[256,1024]{0,1:T(8,128)} %bitcast.1), channel_id=1, source_target_pairs={{0,1},{1,0},{2,3},{3,2},{4,5},{5,4},{6,7},{7,6},{8,9},{9,8},{10,11... | collective-permute-start | bytes 3145736 | tf_op jit(solution)/shard_map/ppermute | solution.py:250
  9.6 15.8 %copy-start.51 = (f32[256,1024]{0,1:T(8,128)}, f32[256,1024]{0,1:T(8,128)S(1)}, u32[]{:S(2)}) copy-start(f32[256,1024]{0,1:T(8,128)S(1)} %collective-permute-done) | copy-start | bytes 3145732
  10.6 18.6 %all-to-all-start = ((f32[32,1,768]{2,1,0:T(1,128)}), f32[32,1,768]{2,1,0:T(1,128)S(1)}, u32[]{:S(2)}, u32[]{:S(2)}) async-start(f32[32,1,768]{2,1,0:T(1,128)} %reshape.92), calls=%async_computation | async-start | bytes 196608 | tf_op jit(solution)/shard_map/all_to_all | solution.py:255
  20.2 4.0 collective-permute-start.1
  24.1 3.6 collective-permute-start.2
  25.8 4.5 %copy-start = (f32[256,1024]{1,0:T(8,128)}, f32[256,1024]{1,0:T(8,128)S(1)}, u32[]{:S(2)}) copy-start(f32[256,1024]{1,0:T(8,128)S(1)} %copy.114.own_ref.refs_0_.refs_1_) | copy-start | bytes 3145732
  27.7 22.5 %copy-start.24 = (f32[256,1024]{1,0:T(8,128)}, f32[256,1024]{1,0:T(8,128)S(1)}, u32[]{:S(2)}) copy-start(f32[256,1024]{1,0:T(8,128)S(1)} %copy.115.oth_ref.refs_1_.refs_2_) | copy-start | bytes 3145732
  30.3 20.0 %copy-start.48 = (f32[16,2048]{1,0:T(8,128)}, f32[16,2048]{1,0:T(8,128)S(1)}, u32[]{:S(2)}) copy-start(f32[16,2048]{1,0:T(8,128)S(1)} %get-tuple-element.131.refs_2_.u_in) | copy-start | bytes 393220
  30.3 20.0 %all-to-all-start.1 = ((f32[32,1,2944]{2,1,0:T(1,128)}), f32[32,1,2944]{2,1,0:T(1,128)S(1)}, u32[]{:S(2)}, u32[]{:S(2)}) async-start(f32[32,1,2944]{2,1,0:T(1,128)} %get-tuple-element.129), calls=%async_computation.1 | async-start | bytes 753664 | tf_op jit(solution)/shard_map/all_to_all | solution.py:273
  50.3 1.2 copy-start.1
  51.5 1.2 copy-start.25
  54.1 2.5 collective-permute-start.3
  56.6 3.6 collective-permute-start.4
  60.3 1.2 copy-start.2
  61.5 1.2 copy-start.26
  80.1 1.2 copy-start.3
  81.4 1.2 copy-start.27
  83.1 2.5 collective-permute-start.5
  85.6 3.6 collective-permute-start.6
  89.2 1.2 copy-start.4
  90.5 1.2 copy-start.28
  106.1 1.2 copy-start.5
  107.4 1.2 copy-start.29
  109.1 2.8 collective-permute-start.7
  111.9 3.6 collective-permute-start.8
  115.5 1.2 copy-start.6
  116.8 1.2 copy-start.30
  132.3 1.2 copy-start.7
  133.5 1.2 copy-start.31
  135.3 3.0 collective-permute-start.9
  138.3 3.9 collective-permute-start.10
  142.2 1.2 copy-start.8
  158.8 1.2 copy-start.9
  161.7 2.5 collective-permute-start.11
  164.3 3.7 collective-permute-start.12
  168.0 1.2 copy-start.10
  184.7 1.2 copy-start.11
  187.6 2.5 collective-permute-start.13
  190.1 3.6 collective-permute-start.14
  193.8 1.2 copy-start.12
  210.6 1.2 copy-start.13
  213.5 2.5 collective-permute-start.15
  216.0 3.6 collective-permute-start.16
  219.7 1.2 copy-start.14
  236.7 1.2 copy-start.15
  239.6 2.5 collective-permute-start.17
  242.2 3.6 collective-permute-start.18
  245.8 1.2 copy-start.16
  263.9 1.2 copy-start.17
  266.9 2.5 collective-permute-start.19
  269.4 3.6 collective-permute-start.20
  273.0 1.2 copy-start.18
  290.6 1.2 copy-start.19
  293.6 2.5 collective-permute-start.21
  296.1 3.6 collective-permute-start.22
  299.7 1.2 copy-start.20
  316.5 1.2 copy-start.21
  319.5 2.8 collective-permute-start.23
  322.3 3.6 collective-permute-start.24
  325.9 1.2 copy-start.22
  342.7 1.2 copy-start.23
  345.6 2.8 collective-permute-start.25
  348.5 4.6 %collective-permute-start.26 = (f32[1,384]{1,0:T(1,128)S(1)}, f32[1,384]{1,0:T(1,128)S(1)}, u32[]{:S(2)}, u32[]{:S(2)}) collective-permute-start(f32[1,384]{1,0:T(1,128)S(1)} %add.138.a_ref), channel_id=1, source_target_pairs={{0,6},{1,7},{2,4},{3,5},{4,2},{5,3},{6,0},{7,1},{8,14},{9,15},{10,... | collective-permute-start | bytes 4616 | tf_op jit(solution)/shard_map/ppermute | solution.py:285
  353.8 44.1 %collective-permute-start.27 = (f32[32,1408]{1,0:T(8,128)S(1)}, f32[32,1408]{1,0:T(8,128)S(1)}, u32[]{:S(2)}, u32[]{:S(2)}) collective-permute-start(f32[32,1408]{1,0:T(8,128)S(1)} %get-tuple-element.254), channel_id=1, source_target_pairs={{0,1},{1,0},{2,3},{3,2},{4,5},{5,4},{6,7},{7,6},{8,9},{9,8},{10,11... | collective-permute-start | bytes 540680 | tf_op jit(solution)/shard_map/ppermute | solution.py:297
  (18 other events, 21.4 us)

commit v2 on v1

--- a/solution.py
+++ b/solution.py
@@ -120,22 +120,44 @@
         new[...] = old[...]
 
 
-def first_kernel(gr_ref, cols_ref, scat_ref, own_ref, oth_ref, msg_ref, c_ref, *state):
+def open_kernel(core_ref, chip_ref, own_ref, oth_ref, slab_ref):
+    slab = jnp.where(core_ref[...] == 0, own_ref[:, :LANES], oth_ref[:, :LANES])
+    slab = jnp.transpose(slab)[:SLOTS]
+    n = slab.shape[1] // LANES
+    slab_ref[...] = jnp.where(wide(chip_ref[...], n) == 0, slab, 0.0)
+
+
+def first_kernel(gr_ref, cols_ref, own_ref, oth_ref, msg_ref, c_ref, *state):
     for ref in state:
         ref[...] = jnp.zeros_like(ref)
-    send_row(0, cols_ref[0:1], gr_ref, own_ref, oth_ref, None, None, msg_ref, c_ref, scat_ref[0])
+    half = own_ref.shape[1]
+    row = jnp.concatenate([own_ref[0:1], oth_ref[0:1]], axis=1)
+    base = 4 * half + LANES
+    send_row(
+        0, cols_ref[0:1], gr_ref, own_ref, oth_ref, None, None, msg_ref.at[:, :, :base], c_ref, row
+    )
+    piece = msg_ref.shape[2] - base
+    for peer in range(msg_ref.shape[0]):
+        for at in range(0, piece, LANES):
+            row, begin = divmod(peer * piece + at, 2 * half)
+            ref = own_ref if begin < half else oth_ref
+            begin %= half
+            msg_ref[peer, :, base + at : base + at + LANES] = ref[row : row + 1, begin : begin + LANES]
 
 
 def column_kernel(
     step, a_ref, b_ref, r_ref, gr_ref, gc_ref, cols_ref, own_ref, oth_ref, v_ref,
-    x_in, u_in, sd_in, msg_ref, c_ref, x_ref, u_ref, sd_ref,
+    x_in, u_in, sd_in, *refs,
 ):
+    piece_ref = refs[0] if step == 1 else None
+    msg_ref, c_ref, x_ref, u_ref, sd_ref = refs[-5:]
     carry((x_in, u_in, sd_in), (x_ref, u_ref, sd_ref))
     sums = a_ref[...] + b_ref[...]
     column = finish_row_side(
         step, sums, r_ref, gr_ref, gc_ref, cols_ref, v_ref, x_ref, u_ref, sd_ref
     )
-    send_row(step, column, gr_ref, own_ref, oth_ref, v_ref, x_ref, msg_ref, c_ref)
+    extra = None if piece_ref is None else piece_ref[...]
+    send_row(step, column, gr_ref, own_ref, oth_ref, v_ref, x_ref, msg_ref, c_ref, extra)
 
 
 def last_kernel(
@@ -158,25 +180,32 @@
 def row_kernel(
     step, recv_ref, c_ref, gr_ref, gc_ref, *refs,
 ):
+    own_ref, oth_ref, u_ref, v_in, y_in, dg_in = refs[:6]
     if step == 0:
-        own_ref, oth_ref, u_ref, v_in, y_in, dg_in, msg_ref, r_ref, v_ref, y_ref, dg_ref, piv_ref = refs
+        msg_ref, r_ref, v_ref, y_ref, dg_ref, piece_ref = refs[6:]
+    elif step == 1:
+        msg_ref, r_ref, v_ref, y_ref, dg_ref, piv_ref = refs[6:]
     else:
-        piv_ref, own_ref, oth_ref, u_ref, v_in, y_in, dg_in, msg_ref, r_ref, v_ref, y_ref, dg_ref = refs
+        piv_ref, msg_ref, r_ref, v_ref, y_ref, dg_ref = refs[6:]
     carry((v_in, y_in, dg_in), (v_ref, y_ref, dg_ref))
     cols = gc_ref.shape[1]
-    summed = recv_ref[0, :, : cols + LANES]
+    base = cols + LANES
+    summed = recv_ref[0, :, :base]
     for peer in range(1, recv_ref.shape[0]):
-        summed = summed + recv_ref[peer, :, : cols + LANES]
+        summed = summed + recv_ref[peer, :, :base]
     if step == 0:
-        piece = recv_ref.shape[2] - cols - LANES
-        piv_ref[TOTAL:, :] = jnp.zeros((SLOTS - TOTAL, cols), F32)
-        for peer in range(recv_ref.shape[0]):
-            for at in range(0, piece, LANES):
-                flat = peer * piece + at
-                row, begin = flat // cols, flat % cols
-                piv_ref[row : row + 1, begin : begin + LANES] = recv_ref[
-                    peer, :, cols + LANES + at : cols + 2 * LANES + at
-                ]
+        pivot = recv_ref[0, :, base : base + cols]
+        piece_ref[...] = recv_ref[0, :, base + cols :]
+    else:
+        if step == 1:
+            piece = recv_ref.shape[2] - base
+            piv_ref[TOTAL:, :] = jnp.zeros((SLOTS - TOTAL, cols), F32)
+            for peer in range(recv_ref.shape[0]):
+                for at in range(0, piece, LANES):
+                    row, begin = divmod(peer * piece + at, cols)
+                    part = recv_ref[peer, :, base + at : base + at + LANES]
+                    piv_ref[row : row + 1, begin : begin + LANES] = part
+        pivot = piv_ref[step : step + 1]
     dots = spread(summed[:, cols:])
     divisor, factor, remain, bidiag = reflect(dots)
     pick, pick2 = dots[AT_PICK : AT_PICK + SLOTS], dots[AT_PICK2 : AT_PICK2 + SLOTS]
@@ -192,7 +221,7 @@
     half = cols // 2
     for begin in range(0, cols, LANES):
         ts = slice(begin, begin + LANES)
-        y_t, u_t, piv_t, gc_t = y_ref[:, ts], u_ref[:, ts], piv_ref[step : step + 1, ts], gc_ref[:, ts]
+        y_t, u_t, piv_t, gc_t = y_ref[:, ts], u_ref[:, ts], pivot[:, ts], gc_ref[:, ts]
         y = factor * (summed[:, ts] / divisor + piv_t * remain - total(one * y_t + two * u_t))
         y = jnp.where(gc_t > step, y, 0.0)
         r = piv_t - total(pick * y_t + pick2 * u_t) - y
@@ -220,6 +249,7 @@
         out_shape=[pltpu.VMEM(s, F32) for s in outs],
         in_specs=[VMEM] * len(ins),
         out_specs=[VMEM] * len(outs),
+        compiler_params=pltpu.CompilerParams(vmem_limit_bytes=2 << 20),
     )(*(pltpu.with_memory_space_constraint(x, pltpu.VMEM) for x in ins))
 
 
@@ -251,46 +281,44 @@
 
     both = 2 * cols
     piece = TOTAL * both // row_devices
-    scat = jnp.concatenate([own[:TOTAL], oth[:TOTAL]], axis=1).reshape(row_devices, 1, piece)
-    scat = lax.all_to_all(scat, "row", split_axis=0, concat_axis=0, tiled=True)
-    slab = jnp.where(core == 0, own[:, :SLOTS], oth[:, :SLOTS]).T
-    slab = jnp.where(chip == 0, slab, 0.0)
+    flags = [jnp.full((1, LANES), place, jnp.int32) for place in (core, chip)]
+    (slab,) = call(open_kernel, "open", (*flags, own, oth), ((SLOTS, rows),))
     slab = slab + lax.ppermute(slab, "col", [(0, 2), (1, 3)])
     first_cols = slab + lax.ppermute(slab, "col", [(0, 6), (1, 7), (2, 4), (3, 5)])
 
     vec_r, vec_c, flag = (SLOTS, rows), (SLOTS, both), (SLOTS, LANES)
     msg = (row_devices, 1, both + LANES)
-    msg_long = (row_devices, 1, both + LANES + piece)
+    msg_first = (row_devices, 1, 2 * both + LANES + piece)
+    msg_second = (row_devices, 1, both + LANES + piece)
     out = call(
         first_kernel,
         "first",
-        (gr, first_cols, scat, own, oth),
-        (msg_long, (1, rows), vec_r, vec_r, vec_c, vec_c, flag, flag),
+        (gr, first_cols, own, oth),
+        (msg_first, (1, rows), vec_r, vec_r, vec_c, vec_c, flag, flag),
     )
     message, column, v, x, y, u, dg, sd = out
-    pivots = None
     for step in range(TOTAL):
         recv = lax.all_to_all(message, "row", split_axis=0, concat_axis=0, tiled=True)
         lead_in = (recv, column, gr, gc)
         state = (own, oth, u, v, y, dg)
         outs = ((1, rows + LANES), (1, both), vec_r, vec_c, flag)
         kernel = functools.partial(row_kernel, step)
+        ins = lead_in + state
         if step == 0:
-            ins, outs = lead_in + state, outs + (vec_c,)
-            message, r, v, y, dg, pivots = call(kernel, "row_step", ins, outs)
+            message, r, v, y, dg, share = call(kernel, "row_step", ins, outs + ((1, piece),))
+        elif step == 1:
+            message, r, v, y, dg, pivots = call(kernel, "row_step", ins, outs + (vec_c,))
         else:
-            ins = lead_in + (pivots,) + state
-            message, r, v, y, dg = call(kernel, "row_step", ins, outs)
+            message, r, v, y, dg = call(kernel, "row_step", ins + (pivots,), outs)
         part = message + lax.ppermute(message, "col", near)
         rest = lax.ppermute(part, "col", far)
         if step + 1 < TOTAL:
             ins = (part, rest, r, gr, gc, first_cols, own, oth, v, x, u, sd)
-            message, column, x, u, sd = call(
-                functools.partial(column_kernel, step + 1),
-                "column_step",
-                ins,
-                (msg, (1, rows), vec_r, vec_c, flag),
-            )
+            if step == 0:
+                ins += (share,)
+            outs = (msg if step else msg_second, (1, rows), vec_r, vec_c, flag)
+            kernel = functools.partial(column_kernel, step + 1)
+            message, column, x, u, sd = call(kernel, "column_step", ins, outs)
     ins = (part, rest, r, gr, gc, first_cols, v, y, dg, x, u, sd)
     packed = (2 * SLOTS, rows + cols + LANES)
     mine, theirs, _, _, _ = call(last_kernel, "last", ins, (packed, packed, vec_r, vec_c, flag))

time: 407 us -> 343 us (0.84)
  local copies, waits for them, and re-layouts: 69.1 us -> 7.29 us
  waiting for transfers between devices: 76.9 us -> 66.1 us
  starting transfers between devices: 81.5 us -> 90.5 us
    unnamed x107 -> x2, local copies, waits for them, and re-layouts: 58.2 us -> 1.36 us
    ppermute x12, starting transfers between devices: 11.1 us -> 29.8 us  [per_device(): rest = lax.ppermute(part, 'col', far)]
    ppermute x12, waiting for transfers between devices: 30.6 us -> 14.3 us  [per_device(): rest = lax.ppermute(part, 'col', far)]
    all_to_all x1 -> x0, starting transfers between devices: 9.5 us -> none  [per_device(): scat = lax.all_to_all(scat, 'row', split_axis=0, concat_axis=0, tiled=True)]
    all_to_all x1, waiting for transfers between devices: 12.2 us -> 17.4 us  [per_device(): lax.all_to_all(message, 'row', split_axis=0, concat_axis=0, tiled=True)]
    pallas_call x25 -> x26, Pallas kernels: 12 us -> 12 us  [call(): pl.pallas_call(kernel, name=name, out_shape=[pltpu.VMEM(s, F32) for s in...]
  transfers between devices with their start and end apart: 30 -> 29, of which waited for: 28 -> 28; matrix products, arithmetic and copies ran while one was open for 2% -> 1% of each run, Pallas kernels for 0% -> 0%
where the time goes in v2:
time: 343 us; the launch traced here: 342 us
  blocking collectives  159 us (46%)
  starting transfers between devices  90.5 us (26%)
  waiting for transfers between devices  66.1 us (19%)
  Pallas kernels  12 us (3%)
  local copies, waits for them, and re-layouts  7.29 us (2%)
  matrix products  3.64 us (1%)
    all_to_all x11, blocking collectives, per_device(): lax.all_to_all(message, 'row', split_axis=0, concat_axis=0, tiled=True)  159 us
    ppermute x1, starting transfers between devices, per_device(): theirs = lax.ppermute(theirs, 'col', swap)  41.2 us
    ppermute x12, starting transfers between devices, per_device(): rest = lax.ppermute(part, 'col', far)  29.8 us
    ppermute x12, waiting for transfers between devices, per_device(): part = message + lax.ppermute(message, 'col', near)  29.6 us
    all_to_all x1, waiting for transfers between devices, per_device(): lax.all_to_all(message, 'row', split_axis=0, concat_axis=0, tiled=True)  17.4 us
    ppermute x12, waiting for transfers between devices, per_device(): rest = lax.ppermute(part, 'col', far)  14.3 us
    pallas_call x26, Pallas kernels, call(): pl.pallas_call(kernel, name=name, out_shape=[pltpu.VMEM(s, F32) for s in...  12 us
    all_to_all x1, starting transfers between devices, per_device(): lax.all_to_all(message, 'row', split_axis=0, concat_axis=0, tiled=True)  11.2 us
  transfers between devices with their start and end apart: 29, of which 28 were waited for; matrix products, arithmetic and copies ran while one was open for 1% of the time, Pallas kernels for 0%

profile of v2, /device:TPU:1, one launch (start us, length us, event | category | flops | bytes accessed | tf_op | source)
XLA Modules:
  0.0 342.2 jit_solution(665229288838884742)
XLA Ops:
  0.6 1.9 slice_select_fusion
  2.6 1.2 copy.7
  3.7 3.2 collective-permute-start
  7.1 2.3 collective-permute-done.oth_ref.refs_1_
  9.5 1.4 collective-permute-start.1
  10.9 0.8 collective-permute-done.1
  11.8 1.3 collective-permute-start.2
  13.1 0.8 collective-permute-done.2
  13.9 1.2 first.1
  15.1 11.2 %all-to-all-start = ((f32[32,1,4992]{2,1,0:T(1,128)}), f32[32,1,4992]{2,1,0:T(1,128)S(1)}, u32[]{:S(2)}, u32[]{:S(2)}) async-start(f32[32,1,4992]{2,1,0:T(1,128)} %get-tuple-element.130), calls=%async_computation | async-start | bytes 1277952 | tf_op jit(solution)/shard_map/all_to_all | solution.py:301
  26.3 17.4 %all-to-all-done.recv_ref = f32[32,1,4992]{2,1,0:T(1,128)S(1)} async-done(((f32[32,1,4992]{2,1,0:T(1,128)}), f32[32,1,4992]{2,1,0:T(1,128)S(1)}, u32[]{:S(2)}, u32[]{:S(2)}) %all-to-all-start) | async-done | bytes 639008 | tf_op jit(solution)/shard_map/all_to_all | solution.py:301
  44.2 1.0 collective-permute-start.3
  45.2 1.7 collective-permute-done.3
  47.0 2.2 collective-permute-start.4
  49.2 1.4 collective-permute-done.4.b_ref
  51.0 17.3 %all_to_all.60.recv_ref = f32[32,1,2944]{2,1,0:T(1,128)S(1)} all-to-all(f32[32,1,2944]{2,1,0:T(1,128)S(1)} %get-tuple-element.142), channel_id=1, replica_groups=mesh['row'=32,'col'=8] {'row'}, dimensions={0} | all-to-all | bytes 753664 | tf_op jit(solution)/shard_map/all_to_all | solution.py:301
  69.1 2.5 collective-permute-done.5
  71.6 2.7 collective-permute-start.6
  74.2 1.0 collective-permute-done.6.b_ref
  75.6 14.5 %all_to_all.61.recv_ref = f32[32,1,2176]{2,1,0:T(1,128)S(1)} all-to-all(f32[32,1,2176]{2,1,0:T(1,128)S(1)} %get-tuple-element.152), channel_id=1, replica_groups=mesh['row'=32,'col'=8] {'row'}, dimensions={0} | all-to-all | bytes 557056 | tf_op jit(solution)/shard_map/all_to_all | solution.py:301
  90.7 2.7 collective-permute-done.7
  93.4 2.4 collective-permute-start.8
  95.8 1.5 collective-permute-done.8.b_ref
  97.7 13.9 %all_to_all.62.recv_ref = f32[32,1,2176]{2,1,0:T(1,128)S(1)} all-to-all(f32[32,1,2176]{2,1,0:T(1,128)S(1)} %get-tuple-element.163), channel_id=1, replica_groups=mesh['row'=32,'col'=8] {'row'}, dimensions={0} | all-to-all | bytes 557056 | tf_op jit(solution)/shard_map/all_to_all | solution.py:301
  112.2 2.7 collective-permute-done.9
  114.9 2.1 collective-permute-start.10
  117.1 1.8 collective-permute-done.10.b_ref
  119.3 13.7 %all_to_all.63.recv_ref = f32[32,1,2176]{2,1,0:T(1,128)S(1)} all-to-all(f32[32,1,2176]{2,1,0:T(1,128)S(1)} %get-tuple-element.173), channel_id=1, replica_groups=mesh['row'=32,'col'=8] {'row'}, dimensions={0} | all-to-all | bytes 557056 | tf_op jit(solution)/shard_map/all_to_all | solution.py:301
  133.7 2.4 collective-permute-done.11
  136.1 2.4 collective-permute-start.12
  138.5 1.2 collective-permute-done.12.b_ref
  140.1 13.9 %all_to_all.64.recv_ref = f32[32,1,2176]{2,1,0:T(1,128)S(1)} all-to-all(f32[32,1,2176]{2,1,0:T(1,128)S(1)} %get-tuple-element.183), channel_id=1, replica_groups=mesh['row'=32,'col'=8] {'row'}, dimensions={0} | all-to-all | bytes 557056 | tf_op jit(solution)/shard_map/all_to_all | solution.py:301
  154.7 2.4 collective-permute-done.13
  157.1 2.5 collective-permute-start.14
  159.6 1.1 collective-permute-done.14.b_ref
  161.1 14.4 %all_to_all.65.recv_ref = f32[32,1,2176]{2,1,0:T(1,128)S(1)} all-to-all(f32[32,1,2176]{2,1,0:T(1,128)S(1)} %get-tuple-element.193), channel_id=1, replica_groups=mesh['row'=32,'col'=8] {'row'}, dimensions={0} | all-to-all | bytes 557056 | tf_op jit(solution)/shard_map/all_to_all | solution.py:301
  176.1 2.4 collective-permute-done.15
  178.5 2.8 collective-permute-start.16
  181.3 1.0 collective-permute-done.16.b_ref
  182.7 15.0 %all_to_all.66.recv_ref = f32[32,1,2176]{2,1,0:T(1,128)S(1)} all-to-all(f32[32,1,2176]{2,1,0:T(1,128)S(1)} %get-tuple-element.203), channel_id=1, replica_groups=mesh['row'=32,'col'=8] {'row'}, dimensions={0} | all-to-all | bytes 557056 | tf_op jit(solution)/shard_map/all_to_all | solution.py:301
  198.3 2.4 collective-permute-done.17
  200.7 2.3 collective-permute-start.18
  203.0 1.3 collective-permute-done.18.b_ref
  204.7 15.1 %all_to_all.67.recv_ref = f32[32,1,2176]{2,1,0:T(1,128)S(1)} all-to-all(f32[32,1,2176]{2,1,0:T(1,128)S(1)} %get-tuple-element.213), channel_id=1, replica_groups=mesh['row'=32,'col'=8] {'row'}, dimensions={0} | all-to-all | bytes 557056 | tf_op jit(solution)/shard_map/all_to_all | solution.py:301
  220.4 2.7 collective-permute-done.19
  223.1 2.4 collective-permute-start.20
  225.5 1.2 collective-permute-done.20.b_ref
  227.1 13.9 %all_to_all.68.recv_ref = f32[32,1,2176]{2,1,0:T(1,128)S(1)} all-to-all(f32[32,1,2176]{2,1,0:T(1,128)S(1)} %get-tuple-element.223), channel_id=1, replica_groups=mesh['row'=32,'col'=8] {'row'}, dimensions={0} | all-to-all | bytes 557056 | tf_op jit(solution)/shard_map/all_to_all | solution.py:301
  241.6 2.7 collective-permute-done.21
  244.4 2.5 collective-permute-start.22
  246.9 1.4 collective-permute-done.22.b_ref
  248.7 13.8 %all_to_all.69.recv_ref = f32[32,1,2176]{2,1,0:T(1,128)S(1)} all-to-all(f32[32,1,2176]{2,1,0:T(1,128)S(1)} %get-tuple-element.233), channel_id=1, replica_groups=mesh['row'=32,'col'=8] {'row'}, dimensions={0} | all-to-all | bytes 557056 | tf_op jit(solution)/shard_map/all_to_all | solution.py:301
  263.1 2.5 collective-permute-done.23
  265.6 2.8 collective-permute-start.24
  268.4 1.3 collective-permute-done.24.b_ref
  270.0 13.8 %all_to_all.70.recv_ref = f32[32,1,2176]{2,1,0:T(1,128)S(1)} all-to-all(f32[32,1,2176]{2,1,0:T(1,128)S(1)} %get-tuple-element.243), channel_id=1, replica_groups=mesh['row'=32,'col'=8] {'row'}, dimensions={0} | all-to-all | bytes 557056 | tf_op jit(solution)/shard_map/all_to_all | solution.py:301
  284.4 2.4 collective-permute-done.25
  286.8 2.6 collective-permute-start.26
  289.4 3.3 reshape.85
  292.7 0.8 last.1
  293.5 41.2 %collective-permute-start.27 = (f32[32,1408]{1,0:T(8,128)S(1)}, f32[32,1408]{1,0:T(8,128)S(1)}, u32[]{:S(2)}, u32[]{:S(2)}) collective-permute-start(f32[32,1408]{1,0:T(8,128)S(1)} %get-tuple-element.256), channel_id=1, source_target_pairs={{0,1},{1,0},{2,3},{3,2},{4,5},{5,4},{6,7},{7,6},{8,9},{9,8},{10,11... | collective-permute-start | bytes 540680 | tf_op jit(solution)/shard_map/ppermute | solution.py:325
  334.9 0.9 collective-permute-done.27
  336.5 3.6 %subtract_select_fusion = f32[2,256,1024]{2,1,0:T(8,128)S(1)} fusion(f32[2,256,1024]{2,1,0:T(8,128)} %reshape.85, pred[256,1024]{1,0:T(8,128)(4,1)S(1)} %broadcast_and_fusion, f32[1,32,1408]{2,1,0:T(8,128)S(1)} %get-tuple-element.266, f32[1,32,1408]{2,1,0:T(8,128)S(1)} %get-tuple-element.265), kind=kOutput, calls=%fused_computation | convolution fusion | flops 202457088 | bytes 5177344 | tf_op jit(solution)/shard_map/mpr,mpc->mrc/dot_general | solution.py:329
  340.2 2.0 reshape.86
  (62 shorter events, 12.8 us)
Async XLA Ops:
  3.7 5.7 %collective-permute-start = (f32[256,1024]{1,0:T(8,128)}, f32[256,1024]{1,0:T(8,128)S(1)}, u32[]{:S(2)}, u32[]{:S(2)}) collective-permute-start(f32[256,1024]{1,0:T(8,128)} %bitcast.9), channel_id=1, source_target_pairs={{0,1},{1,0},{2,3},{3,2},{4,5},{5,4},{6,7},{7,6},{8,9},{9,8},{10,11... | collective-permute-start | bytes 3145736 | tf_op jit(solution)/shard_map/ppermute | solution.py:280
  9.5 2.3 collective-permute-start.1
  11.8 2.1 collective-permute-start.2
  15.1 28.7 %all-to-all-start = ((f32[32,1,4992]{2,1,0:T(1,128)}), f32[32,1,4992]{2,1,0:T(1,128)S(1)}, u32[]{:S(2)}, u32[]{:S(2)}) async-start(f32[32,1,4992]{2,1,0:T(1,128)} %get-tuple-element.130), calls=%async_computation | async-start | bytes 1277952 | tf_op jit(solution)/shard_map/all_to_all | solution.py:301
  44.2 2.7 collective-permute-start.3
  47.0 3.6 %collective-permute-start.4 = (f32[1,384]{1,0:T(1,128)S(1)}, f32[1,384]{1,0:T(1,128)S(1)}, u32[]{:S(2)}, u32[]{:S(2)}) collective-permute-start(f32[1,384]{1,0:T(1,128)S(1)} %add.127.a_ref), channel_id=1, source_target_pairs={{0,6},{1,7},{2,4},{3,5},{4,2},{5,3},{6,0},{7,1},{8,14},{9,15},{10,... | collective-permute-start | bytes 4616 | tf_op jit(solution)/shard_map/ppermute | solution.py:314
  68.7 2.8 collective-permute-start.5
  71.6 3.6 %collective-permute-start.6 = (f32[1,384]{1,0:T(1,128)S(1)}, f32[1,384]{1,0:T(1,128)S(1)}, u32[]{:S(2)}, u32[]{:S(2)}) collective-permute-start(f32[1,384]{1,0:T(1,128)S(1)} %add.128.a_ref), channel_id=1, source_target_pairs={{0,6},{1,7},{2,4},{3,5},{4,2},{5,3},{6,0},{7,1},{8,14},{9,15},{10,... | collective-permute-start | bytes 4616 | tf_op jit(solution)/shard_map/ppermute | solution.py:314
  90.6 2.8 collective-permute-start.7
  93.4 3.9 %collective-permute-start.8 = (f32[1,384]{1,0:T(1,128)S(1)}, f32[1,384]{1,0:T(1,128)S(1)}, u32[]{:S(2)}, u32[]{:S(2)}) collective-permute-start(f32[1,384]{1,0:T(1,128)S(1)} %add.129.a_ref), channel_id=1, source_target_pairs={{0,6},{1,7},{2,4},{3,5},{4,2},{5,3},{6,0},{7,1},{8,14},{9,15},{10,... | collective-permute-start | bytes 4616 | tf_op jit(solution)/shard_map/ppermute | solution.py:314
  112.1 2.8 collective-permute-start.9
  114.9 3.9 %collective-permute-start.10 = (f32[1,384]{1,0:T(1,128)S(1)}, f32[1,384]{1,0:T(1,128)S(1)}, u32[]{:S(2)}, u32[]{:S(2)}) collective-permute-start(f32[1,384]{1,0:T(1,128)S(1)} %add.130.a_ref), channel_id=1, source_target_pairs={{0,6},{1,7},{2,4},{3,5},{4,2},{5,3},{6,0},{7,1},{8,14},{9,15},{10,... | collective-permute-start | bytes 4616 | tf_op jit(solution)/shard_map/ppermute | solution.py:314
  133.4 2.7 collective-permute-start.11
  136.1 3.6 %collective-permute-start.12 = (f32[1,384]{1,0:T(1,128)S(1)}, f32[1,384]{1,0:T(1,128)S(1)}, u32[]{:S(2)}, u32[]{:S(2)}) collective-permute-start(f32[1,384]{1,0:T(1,128)S(1)} %add.131.a_ref), channel_id=1, source_target_pairs={{0,6},{1,7},{2,4},{3,5},{4,2},{5,3},{6,0},{7,1},{8,14},{9,15},{10,... | collective-permute-start | bytes 4616 | tf_op jit(solution)/shard_map/ppermute | solution.py:314
  154.6 2.5 collective-permute-start.13
  157.1 3.6 %collective-permute-start.14 = (f32[1,384]{1,0:T(1,128)S(1)}, f32[1,384]{1,0:T(1,128)S(1)}, u32[]{:S(2)}, u32[]{:S(2)}) collective-permute-start(f32[1,384]{1,0:T(1,128)S(1)} %add.132.a_ref), channel_id=1, source_target_pairs={{0,6},{1,7},{2,4},{3,5},{4,2},{5,3},{6,0},{7,1},{8,14},{9,15},{10,... | collective-permute-start | bytes 4616 | tf_op jit(solution)/shard_map/ppermute | solution.py:314
  176.0 2.5 collective-permute-start.15
  178.5 3.8 %collective-permute-start.16 = (f32[1,384]{1,0:T(1,128)S(1)}, f32[1,384]{1,0:T(1,128)S(1)}, u32[]{:S(2)}, u32[]{:S(2)}) collective-permute-start(f32[1,384]{1,0:T(1,128)S(1)} %add.133.a_ref), channel_id=1, source_target_pairs={{0,6},{1,7},{2,4},{3,5},{4,2},{5,3},{6,0},{7,1},{8,14},{9,15},{10,... | collective-permute-start | bytes 4616 | tf_op jit(solution)/shard_map/ppermute | solution.py:314
  198.2 2.5 collective-permute-start.17
  200.7 3.6 %collective-permute-start.18 = (f32[1,384]{1,0:T(1,128)S(1)}, f32[1,384]{1,0:T(1,128)S(1)}, u32[]{:S(2)}, u32[]{:S(2)}) collective-permute-start(f32[1,384]{1,0:T(1,128)S(1)} %add.134.a_ref), channel_id=1, source_target_pairs={{0,6},{1,7},{2,4},{3,5},{4,2},{5,3},{6,0},{7,1},{8,14},{9,15},{10,... | collective-permute-start | bytes 4616 | tf_op jit(solution)/shard_map/ppermute | solution.py:314
  220.3 2.8 collective-permute-start.19
  223.1 3.6 %collective-permute-start.20 = (f32[1,384]{1,0:T(1,128)S(1)}, f32[1,384]{1,0:T(1,128)S(1)}, u32[]{:S(2)}, u32[]{:S(2)}) collective-permute-start(f32[1,384]{1,0:T(1,128)S(1)} %add.135.a_ref), channel_id=1, source_target_pairs={{0,6},{1,7},{2,4},{3,5},{4,2},{5,3},{6,0},{7,1},{8,14},{9,15},{10,... | collective-permute-start | bytes 4616 | tf_op jit(solution)/shard_map/ppermute | solution.py:314
  241.5 2.8 collective-permute-start.21
  244.4 3.9 %collective-permute-start.22 = (f32[1,384]{1,0:T(1,128)S(1)}, f32[1,384]{1,0:T(1,128)S(1)}, u32[]{:S(2)}, u32[]{:S(2)}) collective-permute-start(f32[1,384]{1,0:T(1,128)S(1)} %add.136.a_ref), channel_id=1, source_target_pairs={{0,6},{1,7},{2,4},{3,5},{4,2},{5,3},{6,0},{7,1},{8,14},{9,15},{10,... | collective-permute-start | bytes 4616 | tf_op jit(solution)/shard_map/ppermute | solution.py:314
  263.0 2.6 collective-permute-start.23
  265.6 4.0 %collective-permute-start.24 = (f32[1,384]{1,0:T(1,128)S(1)}, f32[1,384]{1,0:T(1,128)S(1)}, u32[]{:S(2)}, u32[]{:S(2)}) collective-permute-start(f32[1,384]{1,0:T(1,128)S(1)} %add.137.a_ref), channel_id=1, source_target_pairs={{0,6},{1,7},{2,4},{3,5},{4,2},{5,3},{6,0},{7,1},{8,14},{9,15},{10,... | collective-permute-start | bytes 4616 | tf_op jit(solution)/shard_map/ppermute | solution.py:314
  284.3 2.5 collective-permute-start.25
  286.8 5.9 %collective-permute-start.26 = (f32[1,384]{1,0:T(1,128)S(1)}, f32[1,384]{1,0:T(1,128)S(1)}, u32[]{:S(2)}, u32[]{:S(2)}) collective-permute-start(f32[1,384]{1,0:T(1,128)S(1)} %add.138.a_ref), channel_id=1, source_target_pairs={{0,6},{1,7},{2,4},{3,5},{4,2},{5,3},{6,0},{7,1},{8,14},{9,15},{10,... | collective-permute-start | bytes 4616 | tf_op jit(solution)/shard_map/ppermute | solution.py:314
  293.5 42.3 %collective-permute-start.27 = (f32[32,1408]{1,0:T(8,128)S(1)}, f32[32,1408]{1,0:T(8,128)S(1)}, u32[]{:S(2)}, u32[]{:S(2)}) collective-permute-start(f32[32,1408]{1,0:T(8,128)S(1)} %get-tuple-element.256), channel_id=1, source_target_pairs={{0,1},{1,0},{2,3},{3,2},{4,5},{5,4},{6,7},{7,6},{8,9},{9,8},{10,11... | collective-permute-start | bytes 540680 | tf_op jit(solution)/shard_map/ppermute | solution.py:325
